TPU v7x, 128 devices: a whole 4x4x4 slice. The times are simulated.
128 devices in a mesh: row: 16 (over y, z), col: 8 (over x, core).
Axes of the slice: x: 4, y: 4, z: 4, core: 2. Of those that a mesh axis runs over, the one named last changes fastest.
Arguments:
- densities: bfloat16 [18432, 3072], P(('row', 'col')), may hold values from -0.796875 to 0.796875
- counts: int32 [2048], P(('row', 'col')), may hold values from 3 to 9
- coulomb: float32 [3072], replicated, may hold values from 0.05 to 1
- energies: float32 [18432], P(('row', 'col')), may hold values from 8 to 64
- vectors: bfloat16 [18432, 64], P(('row', 'col')), may hold values from -0.046875 to 0.046875
Outputs:
- kernel: float32 [18432, 18432], P('row', 'col')
- product: float32 [18432, 64], P(('row', 'col'))
All inputs are finite; a program needn't handle non-finite values.
Results may differ from a plain program's by a relative error of at most 0.0095.
Values may be sent and summed in bfloat16 or wider, within the bound.
No kernel may reach another device: no remote copies, remote signals or barrier semaphores. Data moves between devices by JAX's collectives and lax.ppermute only.
A program may use at most 128 MiB of HBM per device.

v0:
```python
import jax
import jax.numpy as jnp
from jax import lax
from jax.sharding import Mesh
from jax.sharding import PartitionSpec as P

SLOT = 9
ROW = ("row_0", "row_1")
ROW_COL = ("row_0", "row_1", "col")


def gather_axes(value, axes, dim):
    filled = value
    for number in range(len(axes) - 1, -1, -1):
        filled = lax.all_gather(filled, axes[number], axis=dim, tiled=True)
    return filled


def split_up(value, dim, count):
    before, after = (value.shape[:dim], value.shape[dim + 1 :])
    return jnp.moveaxis(value.reshape(*before, count, -1, *after), dim, 0)


def sent_and_summed(value, axis, dim):
    count = lax.axis_size(axis)
    blocks = lax.all_to_all(split_up(value, dim, count), axis, 0, 0, tiled=True)
    return jnp.sum(blocks.astype(jnp.float32), axis=0)


def split_product(matrix, right_side):
    high = matrix.astype(jnp.bfloat16)
    rest = matrix - high.astype(jnp.float32)
    middle = rest.astype(jnp.bfloat16)
    lowest = (rest - middle.astype(jnp.float32)).astype(jnp.bfloat16)
    total = jnp.dot(high, right_side, preferred_element_type=jnp.float32)
    total = total + jnp.dot(middle, right_side, preferred_element_type=jnp.float32)
    return total + jnp.dot(lowest, right_side, preferred_element_type=jnp.float32)


def body(densities, counts, coulomb, energies, vectors):
    kpoints = counts.shape[0]
    slot_index = lax.broadcasted_iota(jnp.int32, (kpoints, SLOT), 1)
    usable = (slot_index < counts[:, None]).reshape(kpoints * SLOT)
    masked = jnp.where(usable[:, None], densities, jnp.zeros_like(densities))
    weighted = (masked.astype(jnp.float32) * coulomb[None, :]).astype(jnp.bfloat16)
    row_block = lax.all_gather(weighted, "col", axis=0, tiled=True)
    kernel = lax.dot_general(
        row_block,
        lax.all_gather(masked, ROW, axis=0, tiled=True),
        (((1,), (1,)), ((), ())),
        preferred_element_type=jnp.float32,
    )
    column_vectors = gather_axes(vectors, ROW, 0)
    partial_value = split_product(kernel, column_vectors)
    coupled = sent_and_summed(partial_value.astype(jnp.bfloat16), "col", 0)
    diagonal = jnp.where(usable, energies, jnp.zeros_like(energies))
    product = coupled + diagonal[:, None] * vectors.astype(jnp.float32)
    return (kernel, product)


def solution(mesh):
    finer = Mesh(mesh.devices.reshape(4, 4, mesh.shape["col"]), ("row_0", "row_1", "col"))
    in_specs = (P(ROW_COL, None), P(ROW_COL), P(), P(ROW_COL), P(ROW_COL, None))
    out_specs = (P(ROW, "col"), P(ROW_COL, None))
    return jax.shard_map(body, mesh=finer, in_specs=in_specs, out_specs=out_specs, check_vma=False)
```

profile of v0, /device:TPU:1, one launch (start us, length us, event | category | flops | bytes accessed | tf_op | source)
XLA Modules:
  0.0 206.2 jit_solution(9412224943959909971)
XLA Ops:
  7.2 0.0 all-gather.5.cloned.1.call-start
  7.2 0.7 iota_compare_fusion
  7.9 0.1 lt.18
  8.0 2.8 %multiply_convert_fusion = (bf16[144,3072]{1,0:T(8,128)(2,1)}, bf16[144,3072]{1,0:T(8,128)(2,1)}) fusion(f32[3072]{0:T(1024)} %param.7, bf16[144,3072]{1,0:T(8,128)(2,1)} %param.5, pred[144]{0:T(512)(128)(4,1)S(1)} %lt.18), kind=kLoop, calls=%fused_computation.10 | loop fusion | flops 1769472 | bytes 2666640 | tf_op jit(solution)/shard_map/convert_element_type | solution.py:45
  10.8 0.0 all-gather.5.cloned.1.call-update
  10.8 0.0 all-gather.7.cloned.1.call-start
  10.9 0.7 all-gather.7.cloned.1.call-update
  11.6 11.8 %all-gather = bf16[4,144,64]{1,2,0:T(8,128)(2,1)S(1)} all-gather(bf16[1,144,64]{1,2,0:T(8,128)(2,1)} %bitcast.12), channel_id=1, replica_groups=mesh['row_0'=4,'row_1'=4,'col'=8] {'row_1'}, dimensions={0}, use_global_device_ids=true | all-gather | bytes 92160 | tf_op jit(solution)/shard_map/all_gather | solution.py:15
  23.4 0.1 copy.10
  23.5 0.1 reshape.30
  23.6 11.2 %all-gather.1 = bf16[4,576,64]{1,2,0:T(8,128)(2,1)S(1)} all-gather(bf16[1,576,64]{1,2,0:T(8,128)(2,1)S(1)} %reshape.30), channel_id=1, replica_groups=mesh['row_0'=4,'row_1'=4,'col'=8] {'row_0'}, dimensions={0}, use_global_device_ids=true | all-gather | bytes 368640 | tf_op jit(solution)/shard_map/all_gather | solution.py:15
  34.9 0.3 copy.11
  35.1 0.3 reshape.31
  35.4 23.3 %all-gather.5.cloned.1.call-done = bf16[1152,3072]{1,0:T(8,128)(2,1)} async-done(((bf16[144,3072]{1,0:T(8,128)(2,1)}), bf16[1152,3072]{1,0:T(8,128)(2,1)}) %all-gather.5.cloned.1.call-update) | async-done | bytes 7077904 | tf_op jit(solution)/shard_map/all_gather | solution.py:46
  58.7 99.7 %all-gather.7.cloned.1.call-done = bf16[2304,3072]{1,0:T(8,128)(2,1)} async-done(((bf16[144,3072]{1,0:T(8,128)(2,1)}), bf16[2304,3072]{1,0:T(8,128)(2,1)}) %all-gather.7.cloned.1.call-update) | async-done | bytes 14155792 | tf_op jit(solution)/shard_map/all_gather | solution.py:49
  158.4 21.7 %fusion.11 = f32[1152,2304]{1,0:T(8,128)S(1)} fusion(bf16[1152,3072]{1,0:T(8,128)(2,1)} %all-gather.5.cloned.1.call-done, bf16[2304,3072]{1,0:T(8,128)(2,1)} %all-gather.7.cloned.1.call-done), kind=kOutput, calls=%fused_computation.16 | convolution fusion | flops 16307453952 | bytes 31850496 | tf_op jit(solution)/shard_map/dot_general | solution.py:47
  180.1 0.0 copy-start
  180.1 1.7 fusion.1
  181.9 1.8 fusion.7
  183.6 0.6 copy-done
  184.2 0.0 copy-start.2
  184.2 0.0 copy-start.1
  184.2 1.8 fusion.10
  186.0 0.4 reshape.27
  186.4 0.7 copy.12
  187.1 5.1 %all-to-all-start = ((bf16[8,144,64]{1,2,0:T(8,128)(2,1)}), bf16[8,144,64]{1,2,0:T(8,128)(2,1)S(1)}, u32[]{:S(2)}, u32[]{:S(2)}) async-start(bf16[8,144,64]{1,2,0:T(8,128)(2,1)} %copy.12), calls=%async_computation | async-start | bytes 524288 | tf_op jit(solution)/shard_map/all_to_all | solution.py:26
  192.2 0.0 copy-done.2
  192.2 6.5 %all-to-all-done = bf16[8,144,64]{1,2,0:T(8,128)(2,1)S(1)} async-done(((bf16[8,144,64]{1,2,0:T(8,128)(2,1)}), bf16[8,144,64]{1,2,0:T(8,128)(2,1)S(1)}, u32[]{:S(2)}, u32[]{:S(2)}) %all-to-all-start) | async-done | bytes 147488 | tf_op jit(solution)/shard_map/all_to_all | solution.py:26
  198.8 0.0 copy-done.1
  198.8 0.6 multiply_add_fusion
  (2 shorter events, 0.1 us)
Async XLA Ops:
  7.2 51.6 %all-gather.5.cloned.1.call-start = ((), (), s32[]{:S(2)}) async-start(), calls=%async_computation.1 | async-start | bytes 7962624 | tf_op jit(solution)/shard_map/all_gather | solution.py:46
  10.8 147.6 %all-gather.7.cloned.1.call-start = ((), (), s32[]{:S(2)}) async-start(), calls=%async_computation.2 | async-start | bytes 15040512 | tf_op jit(solution)/shard_map/all_gather | solution.py:49
  180.1 4.1 %copy-start = (f32[1152,2304]{1,0:T(8,128)}, f32[1152,2304]{1,0:T(8,128)S(1)}, u32[]{:S(2)}) copy-start(f32[1152,2304]{1,0:T(8,128)S(1)} %fusion.11) | copy-start | bytes 31850500
  184.2 8.0 %copy-start.2 = (f32[144]{0:T(256)S(1)}, f32[144]{0:T(256)}, u32[]{:S(2)}) copy-start(f32[144]{0:T(256)} %param.8) | copy-start | bytes 1732
  184.2 14.5 %copy-start.1 = (bf16[144,64]{0,1:T(8,128)(2,1)S(1)}, bf16[144,64]{0,1:T(8,128)(2,1)}, u32[]{:S(2)}) copy-start(bf16[144,64]{0,1:T(8,128)(2,1)} %param.9) | copy-start | bytes 55300
  187.1 11.6 %all-to-all-start = ((bf16[8,144,64]{1,2,0:T(8,128)(2,1)}), bf16[8,144,64]{1,2,0:T(8,128)(2,1)S(1)}, u32[]{:S(2)}, u32[]{:S(2)}) async-start(bf16[8,144,64]{1,2,0:T(8,128)(2,1)} %copy.12), calls=%async_computation | async-start | bytes 524288 | tf_op jit(solution)/shard_map/all_to_all | solution.py:26
Sparse Core Ops, SparseCore 0:
  11.0 47.7 all-gather.4
  60.9 97.4 all-gather.6
where the time goes:
time: 207 us; the launch traced here: 206 us
  waiting for transfers between devices  130 us (63%)
  matrix products  27 us (13%)
  blocking collectives  23 us (11%)
  between operations  14.1 us (7%)
  starting transfers between devices  5.17 us (2%)
  other arithmetic  4.2 us (2%)
  local copies, waits for them, and re-layouts  2.6 us (1%)
    all_gather x1, waiting for transfers between devices, body(): lax.all_gather(masked, ROW, axis=0, tiled=True)  99.7 us
    all_gather x1, waiting for transfers between devices, body(): row_block = lax.all_gather(weighted, 'col', axis=0, tiled=True)  23.3 us
    all_gather x2, blocking collectives, gather_axes(): filled = lax.all_gather(filled, axes[number], axis=dim, tiled=True)  23 us
    dot_general x1, matrix products, body(): lax.dot_general(row_block, lax.all_gather(masked, ROW, axis=0, tiled=True...  21.7 us
    all_to_all x1, waiting for transfers between devices, sent_and_summed(): blocks = lax.all_to_all(split_up(value, dim, count), axis, 0, 0, tiled=True)  6.46 us
    all_to_all x1, starting transfers between devices, sent_and_summed(): blocks = lax.all_to_all(split_up(value, dim, count), axis, 0, 0, tiled=True)  5.09 us
  transfers between devices with their start and end apart: 3, of which 3 were waited for; matrix products, arithmetic and copies ran while one was open for 0% of the time, Pallas kernels for 0%

commit v1 on v0

--- a/solution.py
+++ b/solution.py
@@ -43,7 +43,8 @@
     usable = (slot_index < counts[:, None]).reshape(kpoints * SLOT)
     masked = jnp.where(usable[:, None], densities, jnp.zeros_like(densities))
     weighted = (masked.astype(jnp.float32) * coulomb[None, :]).astype(jnp.bfloat16)
-    row_block = lax.all_gather(weighted, "col", axis=0, tiled=True)
+    copies = jnp.concatenate([weighted] * lax.axis_size("col"), axis=0)
+    row_block = lax.all_to_all(copies, "col", 0, 0, tiled=True)
     kernel = lax.dot_general(
         row_block,
         lax.all_gather(masked, ROW, axis=0, tiled=True),

time: 207 us -> 162 us (0.78)
  waiting for transfers between devices: 130 us -> 66.2 us
  other arithmetic: 4.2 us -> 16.6 us
  starting transfers between devices: 5.17 us -> 11.2 us
    all_gather x1, waiting for transfers between devices: 99.7 us -> 4.32 us  [body(): lax.all_gather(masked, ROW, axis=0, tiled=True)]
    all_to_all x0 -> x1, waiting for transfers between devices: none -> 55.4 us  [body(): row_block = lax.all_to_all(copies, 'col', 0, 0, tiled=True)]
    all_gather x1 -> x0, waiting for transfers between devices: 23.3 us -> none  [body(): row_block = lax.all_gather(weighted, 'col', axis=0, tiled=True)]
    unnamed x0 -> x7, other arithmetic: none -> 14 us
    all_to_all x0 -> x1, starting transfers between devices: none -> 6.24 us  [body(): row_block = lax.all_to_all(copies, 'col', 0, 0, tiled=True)]
    convert_element_type x1 -> x0, other arithmetic: 2.78 us -> none  [body(): (masked.astype(jnp.float32) * coulomb[None, :]).astype(jnp.bfloat16)]
  transfers between devices with their start and end apart: 3 -> 3, of which waited for: 3 -> 3; matrix products, arithmetic and copies ran while one was open for 0% -> 8% of each run, Pallas kernels for 0% -> 0%
where the time goes in v1:
time: 162 us; the launch traced here: 161 us
  waiting for transfers between devices  66.2 us (41%)
  matrix products  26.9 us (17%)
  blocking collectives  23.5 us (15%)
  other arithmetic  16.6 us (10%)
  between operations  14.1 us (9%)
  starting transfers between devices  11.2 us (7%)
  local copies, waits for them, and re-layouts  2.63 us (2%)
    all_to_all x1, waiting for transfers between devices, body(): row_block = lax.all_to_all(copies, 'col', 0, 0, tiled=True)  55.4 us
    all_gather x2, blocking collectives, gather_axes(): filled = lax.all_gather(filled, axes[number], axis=dim, tiled=True)  23.5 us
    dot_general x1, matrix products, body(): lax.dot_general(row_block, lax.all_gather(masked, ROW, axis=0, tiled=True...  21.7 us
    unnamed x7, other arithmetic  14 us
    all_to_all x1, waiting for transfers between devices, sent_and_summed(): blocks = lax.all_to_all(split_up(value, dim, count), axis, 0, 0, tiled=True)  6.46 us
    all_to_all x1, starting transfers between devices, body(): row_block = lax.all_to_all(copies, 'col', 0, 0, tiled=True)  6.24 us
    all_to_all x1, starting transfers between devices, sent_and_summed(): blocks = lax.all_to_all(split_up(value, dim, count), axis, 0, 0, tiled=True)  4.88 us
    all_gather x1, waiting for transfers between devices, body(): lax.all_gather(masked, ROW, axis=0, tiled=True)  4.32 us
  transfers between devices with their start and end apart: 3, of which 3 were waited for; matrix products, arithmetic and copies ran while one was open for 8% of the time, Pallas kernels for 0%

profile of v1, /device:TPU:1, one launch (start us, length us, event | category | flops | bytes accessed | tf_op | source)
XLA Modules:
  0.0 161.1 jit_solution(11362092981301030218)
XLA Ops:
  7.2 0.0 copy-start.2
  7.2 0.0 all-gather.4.cloned.1.call-start
  7.2 0.7 iota_compare_fusion
  8.0 0.1 lt.18
  8.1 2.8 %fusion.17 = (bf16[1152,3072]{1,0:T(8,128)(2,1)}, bf16[144,3072]{1,0:T(8,128)(2,1)}) fusion(f32[3072]{0:T(1024)} %param.7, bf16[144,3072]{1,0:T(8,128)(2,1)} %param.5, pred[144]{0:T(512)(128)(4,1)S(1)} %lt.18), kind=kLoop, calls=%fused_computation.19 | loop fusion | flops 1769471 | bytes 2666640
  10.8 0.0 copy-start.1
  10.8 0.0 all-gather.4.cloned.1.call-update
  10.9 2.3 %fusion.16 = bf16[1152,3072]{1,0:T(8,128)(2,1)} fusion(bf16[1152,3072]{1,0:T(8,128)(2,1)} %get-tuple-element.2, f32[3072]{0:T(1024)} %param.7, bf16[144,3072]{1,0:T(8,128)(2,1)} %get-tuple-element.3), kind=kLoop, calls=%fused_computation.18 | loop fusion | flops 1327104 | bytes 1781760
  13.2 2.3 %fusion.15 = bf16[1152,3072]{1,0:T(8,128)(2,1)} fusion(bf16[1152,3072]{1,0:T(8,128)(2,1)} %fusion.16, f32[3072]{0:T(1024)} %param.7, bf16[144,3072]{1,0:T(8,128)(2,1)} %get-tuple-element.3), kind=kLoop, calls=%fused_computation.17 | loop fusion | flops 1327104 | bytes 1781760
  15.5 0.0 copy-done.2
  15.5 2.2 %fusion.14 = bf16[1152,3072]{1,0:T(8,128)(2,1)} fusion(bf16[1152,3072]{1,0:T(8,128)(2,1)} %fusion.15, f32[3072]{0:T(1024)S(1)} %copy-done.2, bf16[144,3072]{1,0:T(8,128)(2,1)} %get-tuple-element.3), kind=kLoop, calls=%fused_computation.16 | loop fusion | flops 1327104 | bytes 1781760
  17.7 2.2 %fusion.13 = bf16[1152,3072]{1,0:T(8,128)(2,1)} fusion(bf16[1152,3072]{1,0:T(8,128)(2,1)} %fusion.14, f32[3072]{0:T(1024)S(1)} %copy-done.2, bf16[144,3072]{1,0:T(8,128)(2,1)} %get-tuple-element.3), kind=kLoop, calls=%fused_computation.15 | loop fusion | flops 1327104 | bytes 1781760
  20.0 0.0 copy-done.1
  20.0 1.1 fusion.12
  21.0 1.1 fusion.11
  22.1 1.1 fusion.18
  23.2 0.0 copy-start.3
  23.2 6.2 %all-to-all-start = ((bf16[8,144,3072]{2,1,0:T(8,128)(2,1)}), bf16[8,144,3072]{2,1,0:T(8,128)(2,1)}, u32[]{:S(2)}, u32[]{:S(2)}) async-start(bf16[8,144,3072]{2,1,0:T(8,128)(2,1)} %bitcast.14), calls=%async_computation | async-start | bytes 14155776 | tf_op jit(solution)/shard_map/all_to_all | solution.py:47
  29.5 0.0 copy-done.3
  29.5 12.1 %all-gather = bf16[4,144,64]{1,2,0:T(8,128)(2,1)S(1)} all-gather(bf16[1,144,64]{1,2,0:T(8,128)(2,1)S(1)} %bitcast.15), channel_id=1, replica_groups=mesh['row_0'=4,'row_1'=4,'col'=8] {'row_1'}, dimensions={0}, use_global_device_ids=true | all-gather | bytes 92160 | tf_op jit(solution)/shard_map/all_gather | solution.py:15
  41.6 0.1 copy.10
  41.7 0.1 reshape.32
  41.9 11.3 %all-gather.1 = bf16[4,576,64]{1,2,0:T(8,128)(2,1)S(1)} all-gather(bf16[1,576,64]{1,2,0:T(8,128)(2,1)S(1)} %reshape.32), channel_id=1, replica_groups=mesh['row_0'=4,'row_1'=4,'col'=8] {'row_0'}, dimensions={0}, use_global_device_ids=true | all-gather | bytes 368640 | tf_op jit(solution)/shard_map/all_gather | solution.py:15
  53.2 0.3 copy.11
  53.4 0.3 reshape.33
  53.7 55.4 %all-to-all-done = bf16[8,144,3072]{2,1,0:T(8,128)(2,1)} async-done(((bf16[8,144,3072]{2,1,0:T(8,128)(2,1)}), bf16[8,144,3072]{2,1,0:T(8,128)(2,1)}, u32[]{:S(2)}, u32[]{:S(2)}) %all-to-all-start) | async-done | bytes 7077920 | tf_op jit(solution)/shard_map/all_to_all | solution.py:47
  109.2 4.3 %all-gather.4.cloned.1.call-done = bf16[2304,3072]{1,0:T(8,128)(2,1)} async-done(((bf16[144,3072]{1,0:T(8,128)(2,1)}), bf16[2304,3072]{1,0:T(8,128)(2,1)}) %all-gather.4.cloned.1.call-update) | async-done | bytes 14155792 | tf_op jit(solution)/shard_map/all_gather | solution.py:50
  113.5 21.7 %fusion.19 = f32[1152,2304]{1,0:T(8,128)S(1)} fusion(bf16[1152,3072]{1,0:T(8,128)(2,1)} %bitcast.1, bf16[2304,3072]{1,0:T(8,128)(2,1)} %all-gather.4.cloned.1.call-done), kind=kOutput, calls=%fused_computation.24 | convolution fusion | flops 16307453952 | bytes 31850496 | tf_op jit(solution)/shard_map/dot_general | solution.py:48
  135.2 0.0 copy-start
  135.2 1.7 %fusion.1 = f32[1152,64]{0,1:T(8,128)S(1)} fusion(bf16[2304,64]{0,1:T(8,128)(2,1)S(1)} %reshape.33, f32[1152,2304]{1,0:T(8,128)S(1)} %fusion.19), kind=kOutput, calls=%fused_computation.3 | convolution fusion | flops 342392832 | bytes 11206656 | tf_op jit(solution)/shard_map/dot_general | solution.py:35
  136.9 1.8 %fusion.7 = f32[1152,64]{0,1:T(8,128)S(1)} fusion(f32[1152,64]{0,1:T(8,128)S(1)} %fusion.1, bf16[2304,64]{0,1:T(8,128)(2,1)S(1)} %reshape.33, f32[1152,2304]{1,0:T(8,128)S(1)} %fusion.19), kind=kOutput, calls=%fused_computation.8 | convolution fusion | flops 350429184 | bytes 11501568 | tf_op jit(solution)/shard_map/dot_general | solution.py:36
  138.7 0.6 copy-done
  139.3 0.0 copy-start.4
  139.3 1.8 %fusion.10 = bf16[1152,64]{0,1:T(8,128)(2,1)S(1)} fusion(f32[1152,64]{0,1:T(8,128)S(1)} %fusion.7, bf16[2304,64]{0,1:T(8,128)(2,1)S(1)} %reshape.33, f32[1152,2304]{1,0:T(8,128)S(1)} %fusion.19), kind=kOutput, calls=%fused_computation.9 | convolution fusion | flops 358465536 | bytes 11354112 | tf_op jit(solution)/shard_map/dot_general | solution.py:37
  141.1 0.4 reshape.29
  141.4 0.8 copy.12
  142.2 4.9 %all-to-all-start.1 = ((bf16[8,144,64]{1,2,0:T(8,128)(2,1)}), bf16[8,144,64]{1,2,0:T(8,128)(2,1)S(1)}, u32[]{:S(2)}, u32[]{:S(2)}) async-start(bf16[8,144,64]{1,2,0:T(8,128)(2,1)} %copy.12), calls=%async_computation.1 | async-start | bytes 524288 | tf_op jit(solution)/shard_map/all_to_all | solution.py:26
  147.1 0.0 copy-done.4
  147.1 6.5 %all-to-all-done.1 = bf16[8,144,64]{1,2,0:T(8,128)(2,1)S(1)} async-done(((bf16[8,144,64]{1,2,0:T(8,128)(2,1)}), bf16[8,144,64]{1,2,0:T(8,128)(2,1)S(1)}, u32[]{:S(2)}, u32[]{:S(2)}) %all-to-all-start.1) | async-done | bytes 147488 | tf_op jit(solution)/shard_map/all_to_all | solution.py:26
  153.6 0.6 multiply_add_fusion
  (2 shorter events, 0.1 us)
Async XLA Ops:
  7.2 8.3 %copy-start.2 = (f32[3072]{0:T(1024)S(1)}, f32[3072]{0:T(1024)}, u32[]{:S(2)}) copy-start(f32[3072]{0:T(1024)} %param.7) | copy-start | bytes 36868
  7.2 106.3 %all-gather.4.cloned.1.call-start = ((), (), s32[]{:S(2)}) async-start(), calls=%async_computation.2 | async-start | bytes 15040512 | tf_op jit(solution)/shard_map/all_gather | solution.py:50
  10.8 9.1 %copy-start.1 = (bf16[144,3072]{1,0:T(8,128)(2,1)S(1)}, bf16[144,3072]{1,0:T(8,128)(2,1)}, u32[]{:S(2)}) copy-start(bf16[144,3072]{1,0:T(8,128)(2,1)} %get-tuple-element.3) | copy-start | bytes 2654212
  23.2 6.2 %copy-start.3 = (bf16[144,64]{0,1:T(8,128)(2,1)S(1)}, bf16[144,64]{0,1:T(8,128)(2,1)}, u32[]{:S(2)}) copy-start(bf16[144,64]{0,1:T(8,128)(2,1)} %param.9) | copy-start | bytes 55300
  23.2 86.0 %all-to-all-start = ((bf16[8,144,3072]{2,1,0:T(8,128)(2,1)}), bf16[8,144,3072]{2,1,0:T(8,128)(2,1)}, u32[]{:S(2)}, u32[]{:S(2)}) async-start(bf16[8,144,3072]{2,1,0:T(8,128)(2,1)} %bitcast.14), calls=%async_computation | async-start | bytes 14155776 | tf_op jit(solution)/shard_map/all_to_all | solution.py:47
  135.2 4.1 %copy-start = (f32[1152,2304]{1,0:T(8,128)}, f32[1152,2304]{1,0:T(8,128)S(1)}, u32[]{:S(2)}) copy-start(f32[1152,2304]{1,0:T(8,128)S(1)} %fusion.19) | copy-start | bytes 31850500
  139.3 7.8 %copy-start.4 = (f32[144]{0:T(256)S(1)}, f32[144]{0:T(256)}, u32[]{:S(2)}) copy-start(f32[144]{0:T(256)} %param.8) | copy-start | bytes 1732
  142.2 11.3 %all-to-all-start.1 = ((bf16[8,144,64]{1,2,0:T(8,128)(2,1)}), bf16[8,144,64]{1,2,0:T(8,128)(2,1)S(1)}, u32[]{:S(2)}, u32[]{:S(2)}) async-start(bf16[8,144,64]{1,2,0:T(8,128)(2,1)} %copy.12), calls=%async_computation.1 | async-start | bytes 524288 | tf_op jit(solution)/shard_map/all_to_all | solution.py:26
Sparse Core Ops, SparseCore 0:
  11.0 102.4 all-gather.3
